TPU v7x, 128 devices: a whole 4x4x4 slice. The times are simulated.
128 devices in a mesh: row: 64 (over y, x, z_hi, core), col: 2 (over z_lo).
Axes of the slice: x: 4, y: 4, z: 4 (z_hi: 2, z_lo: 2; z = z_hi * 2 + z_lo), core: 2. Of those that a mesh axis runs over, the one named last changes fastest.
Arguments:
- tokens: bfloat16 [1024, 8192], P('row', 'col'), may hold values from -6 to 6
- norm_gain: float32 [8192], P('col'), may hold values from 0.1 to 1.9
- gate_weight: bfloat16 [8192, 28672], P('col', 'row'), may hold values from -0.0625 to 0.0625
- up_weight: bfloat16 [8192, 28672], P('col', 'row'), may hold values from -0.0625 to 0.0625
- down_weight: bfloat16 [28672, 8192], P('row', 'col'), may hold values from -0.03125 to 0.03125
Outputs:
- mixed: bfloat16 [1024, 8192], P('row', 'col')
All inputs are finite; a program needn't handle non-finite values.
Results may differ from a plain program's by a relative error of at most 0.0065.
Values may be sent and summed in bfloat16 or wider, within the bound.
A program may use at most 128 MiB of HBM per device.

v0:
```python
import jax
import jax.numpy as jnp
from jax import lax
from jax.sharding import Mesh
from jax.sharding import PartitionSpec as P

D = 8192
ROW = ("row_0", "row_1", "row_2", "row_3")


def copy_for_each(x, axis):
    copies = jnp.broadcast_to(x, (lax.axis_size(axis), *x.shape))
    return lax.all_to_all(copies, axis, split_axis=0, concat_axis=0, tiled=True)


def taken_together(x, axis):
    everything = copy_for_each(x, axis)
    return jnp.sum(everything, axis=0)


def in_blocks(x, dim, count):
    before, after = (x.shape[:dim], x.shape[dim + 1 :])
    return jnp.moveaxis(x.reshape(*before, count, -1, *after), dim, 0)


def sum_at_owner(x, axis, dim):
    count = lax.axis_size(axis)
    blocks = lax.all_to_all(in_blocks(x, dim, count), axis, 0, 0, tiled=True)
    return jnp.sum(blocks, axis=0)


def in_order(blocks, dim):
    blocks = jnp.moveaxis(blocks, 0, dim)
    dims = blocks.shape
    return blocks.reshape(*dims[:dim], dims[dim] * dims[dim + 1], *dims[dim + 2 :])


def collect(x, axis, dim):
    blocks = copy_for_each(x, axis)
    return in_order(blocks, dim)


def summed_rows(x, chips, core, dim):
    sizes = (lax.axis_size(chips), lax.axis_size(core))
    blocks = in_blocks(x, dim, sizes[0] * sizes[1])
    inside = blocks.shape[1:]
    blocks = blocks.reshape(*sizes, *inside).swapaxes(0, 1).reshape(-1, *inside)
    blocks = lax.psum_scatter(blocks, core, scatter_dimension=0, tiled=True)
    return lax.psum_scatter(blocks, chips, scatter_dimension=0, tiled=True)[0]


def gated(both, width):
    return (jax.nn.silu(both[:, :width]) * both[:, width:]).astype(jnp.bfloat16)


def on_device(tokens, norm_gain, gate_weight, up_weight, down_weight):
    widened = tokens.astype(jnp.float32)
    squares = taken_together(jnp.sum(widened * widened, axis=1, keepdims=True), "col")
    normed = (widened * norm_gain[None, :] / jnp.sqrt(squares / D + 1e-05)).astype(jnp.bfloat16)
    width = gate_weight.shape[1]
    piece = lax.all_gather(normed, ROW, axis=0, tiled=True)
    gate_part = jnp.dot(piece, gate_weight, preferred_element_type=jnp.float32)
    up_part = jnp.dot(piece, up_weight, preferred_element_type=jnp.float32)
    partial_value = jnp.concatenate([gate_part, up_part], axis=1)
    shares = sum_at_owner(partial_value, "col", 0)
    hidden = collect(gated(shares, width), "col", 0)
    mixed = summed_rows(
        jnp.dot(hidden, down_weight, preferred_element_type=jnp.float32),
        ("row_0", "row_1", "row_2"),
        "row_3",
        0,
    )
    return mixed.astype(jnp.bfloat16)


def solution(mesh):
    finer = Mesh(
        mesh.devices.reshape(4, 4, 2, 2, mesh.shape["col"]),
        ("row_0", "row_1", "row_2", "row_3", "col"),
    )
    placed = (P(ROW, "col"), P("col"), P("col", ROW), P("col", ROW), P(ROW, "col"))
    return jax.shard_map(
        on_device, mesh=finer, in_specs=placed, out_specs=P(ROW, "col"), check_vma=False
    )
```

profile of v0, /device:TPU:0, one launch (start us, length us, event | category | flops | bytes accessed | tf_op | source)
XLA Modules:
  0.0 435.2 jit_solution(14296491897519222040)
XLA Ops:
  6.5 1.0 fusion.4
  7.6 6.9 %all_to_all.15 = f32[2,16,1]{1,2,0:T(1,128)S(1)} all-to-all(f32[2,16,1]{1,2,0:T(1,128)S(1)} %broadcast_in_dim.8), channel_id=1, replica_groups=mesh['row_0'=4,'row_1'=4,'row_2'=2,'row_3'=2,'col'=2] {'col'}, dimensions={0} | all-to-all | bytes 256 | tf_op jit(solution)/shard_map/all_to_all | solution.py:13
  14.5 1.7 fusion.3
  16.2 0.0 all-gather.2.cloned.1.call-update
  16.2 0.0 reduce-scatter.3.cloned.1.call-start
  16.2 85.4 %all-gather.2.cloned.1.call-done = bf16[1024,4096]{1,0:T(8,128)(2,1)} async-done(((bf16[16,4096]{1,0:T(8,128)(2,1)}), bf16[1024,4096]{1,0:T(8,128)(2,1)}) %all-gather.2.cloned.1.call-update) | async-done | bytes 8388624 | tf_op jit(solution)/shard_map/all_gather | solution.py:61
  101.6 7.7 %fusion.6 = f32[1024,448]{0,1:T(8,128)S(1)} fusion(bf16[1024,4096]{1,0:T(8,128)(2,1)} %all-gather.2.cloned.1.call-done, bf16[4096,448]{0,1:T(8,128)(2,1)} %param.8), kind=kOutput, calls=%fused_computation.14 | convolution fusion | flops 3758096384 | bytes 13893632 | tf_op jit(solution)/shard_map/dot_general | solution.py:63
  109.3 0.2 copy-done.1
  109.5 4.0 fusion.5
  113.5 0.5 pad_maximum_fusion
  114.0 0.5 copy.17
  114.5 46.0 %all_to_all.16 = f32[2,512,896]{1,2,0:T(8,128)} all-to-all(f32[2,512,896]{1,2,0:T(8,128)S(1)} %bitcast.22), channel_id=1, replica_groups=mesh['row_0'=4,'row_1'=4,'row_2'=2,'row_3'=2,'col'=2] {'col'}, dimensions={0} | all-to-all | bytes 7340032 | tf_op jit(solution)/shard_map/all_to_all | solution.py:28
  160.5 2.6 reduce_sum.29
  163.1 0.3 fusion.1
  163.4 0.1 broadcast_in_dim.9
  163.5 14.5 %all_to_all.17 = bf16[2,512,448]{1,2,0:T(8,128)(2,1)S(1)} all-to-all(bf16[2,512,448]{1,2,0:T(8,128)(2,1)S(1)} %broadcast_in_dim.9), channel_id=1, replica_groups=mesh['row_0'=4,'row_1'=4,'row_2'=2,'row_3'=2,'col'=2] {'col'}, dimensions={0} | all-to-all | bytes 1835008 | tf_op jit(solution)/shard_map/all_to_all | solution.py:13
  177.9 0.5 copy.9
  178.4 6.6 %convolution_bitcast_fusion = f32[2,32,16,4096]{3,2,0,1:T(8,128)S(1)} fusion(bf16[32,2,16,448]{3,2,1,0:T(8,128)(2,1)S(1)} %bitcast.23, bf16[448,4096]{1,0:T(8,128)(2,1)} %param.9), kind=kOutput, calls=%fused_computation | convolution fusion | flops 3758096384 | bytes 21364736 | tf_op jit(solution)/shard_map/dot_general | solution.py:68
  185.0 6.0 %copy.10 = f32[2,32,16,4096]{3,2,1,0:T(8,128)} copy(f32[2,32,16,4096]{3,2,0,1:T(8,128)S(1)} %convolution_bitcast_fusion) | data formatting | bytes 33554432 | tf_op jit(solution)/shard_map/transpose | solution.py:47
  191.0 0.0 reduce-scatter.3.cloned.1.call-update
  191.0 0.0 reduce-scatter.5.cloned.1.call-start
  191.1 24.7 %reduce-scatter.3.cloned.1.call-done = f32[32,16,4096]{2,1,0:T(8,128)} async-done(((f32[64,16,4096]{2,1,0:T(8,128)}), f32[32,16,4096]{2,1,0:T(8,128)}) %reduce-scatter.3.cloned.1.call-update) | async-done | bytes 8388624 | tf_op jit(solution)/shard_map/reduce_scatter | solution.py:48
  215.8 211.3 %reduce-scatter.5.cloned.1.call-done = f32[1,16,4096]{2,1,0:T(8,128)} async-done(((f32[32,16,4096]{2,1,0:T(8,128)}), f32[1,16,4096]{2,1,0:T(8,128)}) %reduce-scatter.5.cloned.1.call-update) | async-done | bytes 262160 | tf_op jit(solution)/shard_map/reduce_scatter | solution.py:49
  427.0 1.6 convert_bitcast_fusion
  (8 shorter events, 0.1 us)
Async XLA Ops:
  6.5 95.1 %all-gather.2.cloned.1.call-start = ((), (), s32[]{:S(2)}) async-start(), calls=%async_computation.5 | async-start | bytes 8519680 | tf_op jit(solution)/shard_map/all_gather | solution.py:61
  16.2 199.6 %reduce-scatter.3.cloned.1.call-start = ((), (), s32[]{:S(2)}) async-start(), calls=%async_computation.6 | async-start | bytes 25165824 | tf_op jit(solution)/shard_map/reduce_scatter | solution.py:48
  101.6 7.7 %copy-start = (bf16[1024,4096]{1,0:T(8,128)(2,1)S(1)}, bf16[1024,4096]{1,0:T(8,128)(2,1)}, u32[]{:S(2)}) copy-start(bf16[1024,4096]{1,0:T(8,128)(2,1)} %all-gather.2.cloned.1.call-done) | copy-start | bytes 25165828
  101.6 7.9 %copy-start.1 = (bf16[4096,448]{0,1:T(8,128)(2,1)S(1)}, bf16[4096,448]{0,1:T(8,128)(2,1)}, u32[]{:S(2)}) copy-start(bf16[4096,448]{0,1:T(8,128)(2,1)} %param.7) | copy-start | bytes 11010052
  191.0 236.0 %reduce-scatter.5.cloned.1.call-start = ((), (), s32[]{:S(2)}) async-start(), calls=%async_computation.7 | async-start | bytes 8650752 | tf_op jit(solution)/shard_map/reduce_scatter | solution.py:49
Sparse Core Ops, SparseCore 0:
  16.3 85.2 all-gather.1
  191.2 24.5 reduce-scatter.2
  218.2 208.8 reduce-scatter.4
where the time goes:
time: 436 us; the launch traced here: 435 us
  waiting for transfers between devices  321 us (74%)
  blocking collectives  67.4 us (15%)
  matrix products  18.2 us (4%)
  between operations  13.2 us (3%)
  other arithmetic  7.72 us (2%)
  local copies, waits for them, and re-layouts  7.32 us (2%)
    reduce_scatter x1, waiting for transfers between devices, summed_rows(): return lax.psum_scatter(blocks, chips, scatter_dimension=0, tiled=True)[0]  211 us
    all_gather x1, waiting for transfers between devices, on_device(): piece = lax.all_gather(normed, ROW, axis=0, tiled=True)  85.4 us
    all_to_all x1, blocking collectives, sum_at_owner(): blocks = lax.all_to_all(in_blocks(x, dim, count), axis, 0, 0, tiled=True)  46 us
    reduce_scatter x1, waiting for transfers between devices, summed_rows(): blocks = lax.psum_scatter(blocks, core, scatter_dimension=0, tiled=True)  24.7 us
    all_to_all x2, blocking collectives, copy_for_each(): return lax.all_to_all(copies, axis, split_axis=0, concat_axis=0, tiled=True)  21.3 us
  transfers between devices with their start and end apart: 3, of which 3 were waited for; matrix products, arithmetic and copies ran while one was open for 0% of the time, Pallas kernels for 0%

commit v1 on v0

v1 whole, which is shorter than its diff:
```python
import jax
import jax.numpy as jnp
from jax import lax
from jax.experimental import pallas as pl
from jax.experimental.pallas import tpu as pltpu
from jax.sharding import PartitionSpec as P

D = 8192
BF = jnp.bfloat16
F32 = jnp.float32
MESH = pl.DeviceIdType.MESH
CHUNKS = 4
EARLY, LATE = 0, 1


def layer(tok, gain, wg, wu, wd, out, x, wgu, wdn, tokv, tokp, gainv, sq, sqr,
          acc, bsend, brecv, hid, psend, precv, pown, part, rxa, ta, ua, rxb, tb,
          fown, zsend, zrecv, osend, orecv,
          loc, pre_s, pre_r, ag_s, ag_r, za_s, za_r, fw_s, fw_r, b_s, b_r, c_s, c_r,
          p_s, p_r, ra_s, ra_r, rb_s, rb_r, zr_s, zr_r, o_s, o_r):
    me = lax.axis_index("row")
    c = lax.axis_index("col")
    core = me % 2
    zh = (me // 2) % 2
    xx = (me // 4) % 4
    yy = me // 16
    other = 1 - core

    def row_at(y, x_, z, k):
        return ((y * 4 + x_) * 2 + z) * 2 + k

    mate = {"row": row_at(yy, xx, zh, other), "col": c}
    pair = {"row": me, "col": 1 - c}
    pair_mate = {"row": row_at(yy, xx, zh, other), "col": 1 - c}
    far = {"row": row_at(yy, xx, 1 - zh, core), "col": c}
    xs = tuple({"row": row_at(yy, (xx + d) % 4, zh, core), "col": c} for d in (3, 1))
    ys = tuple({"row": row_at((yy + d) % 4, xx, zh, core), "col": c} for d in (3, 1))

    pending = []

    def send(src, dst, ssem, rsem, to):
        copy = pltpu.make_async_remote_copy(
            src_ref=src, dst_ref=dst, send_sem=ssem, recv_sem=rsem,
            device_id=to, device_id_type=MESH)
        copy.start()
        pending.append(copy)

    def arrived(dst, ssem, rsem, frm):
        pltpu.make_async_remote_copy(
            src_ref=dst, dst_ref=dst, send_sem=ssem, recv_sem=rsem,
            device_id=frm, device_id_type=MESH).wait_recv()

    tok_in = [pltpu.make_async_copy(tok.at[:, pl.ds(1024 * q, 1024)], tokv.at[q], loc.at[q]) for q in range(4)]
    gain_in = [pltpu.make_async_copy(gain.at[:, pl.ds(1024 * q, 1024)], gainv.at[q], loc.at[4 + q]) for q in range(4)]
    w_in = [pltpu.make_async_copy(wg, wgu.at[0], loc.at[8]),
            pltpu.make_async_copy(wu, wgu.at[1], loc.at[9])]
    w_in += [pltpu.make_async_copy(wd.at[:, pl.ds(1024 * q, 1024)], wdn.at[q], loc.at[10 + q]) for q in range(4)]
    for copy in tok_in + gain_in + w_in:
        copy.start()

    barrier = pltpu.get_barrier_semaphore()
    friends = (mate, pair, pair_mate, far) + xs + ys
    for friend in friends:
        pl.semaphore_signal(barrier, inc=1, device_id=friend, device_id_type=MESH)

    for copy in tok_in:
        copy.wait()
    total = jnp.zeros((16, 128), F32)
    for q in range(4):
        for i in range(8):
            v = tokv[q, :, 128 * i:128 * i + 128].astype(F32)
            total = total + v * v
    sq[...] = total

    pl.semaphore_wait(barrier, len(friends))

    send(sq, sqr.at[0], pre_s.at[0], pre_r.at[0], mate)
    send(sq, sqr.at[1], pre_s.at[1], pre_r.at[1], pair)
    send(sq, sqr.at[2], pre_s.at[2], pre_r.at[2], pair_mate)
    send(tokv.at[pl.ds(2 * other, 2)], tokp, pre_s.at[3], pre_r.at[3], mate)
    for copy in gain_in:
        copy.wait()
    arrived(sqr.at[1], pre_s.at[1], pre_r.at[1], pair)
    inv_own = 1.0 / jnp.sqrt(jnp.sum(sq[...] + sqr[1], axis=1, keepdims=True) / D + 1e-05)
    for s in range(2):
        q = 2 * core + s
        x[q, core, yy, xx] = (tokv[q].astype(F32) * gainv[q] * inv_own).astype(BF)
    arrived(sqr.at[0], pre_s.at[0], pre_r.at[0], mate)
    arrived(sqr.at[2], pre_s.at[2], pre_r.at[2], pair_mate)
    arrived(tokp, pre_s.at[3], pre_r.at[3], mate)
    inv_mate = 1.0 / jnp.sqrt(jnp.sum(sqr[0] + sqr[2], axis=1, keepdims=True) / D + 1e-05)
    for s in range(2):
        q = 2 * core + s
        x[q, other, yy, xx] = (tokp[s].astype(F32) * gainv[q] * inv_mate).astype(BF)

    first = (xs, ys)
    second = (ys, xs)
    pcoord = (xx, yy)
    rcoord = (yy, xx)

    def rows_of(ref, s, r):
        return ref.at[r] if s == 0 else ref.at[:, r]

    def xblock(j, s, p):
        return x.at[2 * core + s, j, yy, p] if s == 0 else x.at[2 * core + s, j, p, xx]

    def xrow(j, s, r):
        return rows_of(x.at[2 * core + s, j], s, r)

    def forward(j, s, d):
        r = (rcoord[s] + d) % 4
        send(xrow(j, s, r), xrow(j, s, r), fw_s.at[j, s, d], fw_r.at[j, s, d], mate)

    def forwarded(j):
        for s in range(2):
            for d in range(4):
                q = 2 * other + s
                r = (rcoord[s] + d) % 4
                arrived(rows_of(x.at[q, j], s, r), fw_s.at[j, s, d], fw_r.at[j, s, d], mate)

    def cols(ref, h):
        return ref.at[..., pl.ds(512 * h, 512)]

    def g_start(view, j, s, base, here, to):
        send(view(j, s, here), view(j, s, here), ag_s.at[j, s, base], ag_r.at[j, s, base], to[1])
        send(view(j, s, here), view(j, s, here), ag_s.at[j, s, base + 1], ag_r.at[j, s, base + 1], to[0])

    def g_relay(view, j, s, base, here, to):
        low, high = (here + 3) % 4, (here + 1) % 4
        arrived(view(j, s, low), ag_s.at[j, s, base], ag_r.at[j, s, base], to[0])
        send(cols(view(j, s, low), 0), cols(view(j, s, low), 0),
             ag_s.at[j, s, base + 2], ag_r.at[j, s, base + 2], to[1])
        arrived(view(j, s, high), ag_s.at[j, s, base + 1], ag_r.at[j, s, base + 1], to[1])
        send(cols(view(j, s, high), 1), cols(view(j, s, high), 1),
             ag_s.at[j, s, base + 3], ag_r.at[j, s, base + 3], to[0])

    def g_last(view, j, s, base, here, to):
        opp = (here + 2) % 4
        arrived(cols(view(j, s, opp), 0), ag_s.at[j, s, base + 2], ag_r.at[j, s, base + 2], to[0])
        arrived(cols(view(j, s, opp), 1), ag_s.at[j, s, base + 3], ag_r.at[j, s, base + 3], to[1])

    def a1(j):
        for s in range(2):
            g_start(xblock, j, s, 0, pcoord[s], first[s])

    def a2(j):
        for s in range(2):
            g_relay(xblock, j, s, 0, pcoord[s], first[s])

    def a3(j):
        for s in range(2):
            g_last(xblock, j, s, 0, pcoord[s], first[s])
            g_start(xrow, j, s, 4, rcoord[s], second[s])
            forward(j, s, 0)

    def a4(j):
        for s in range(2):
            g_relay(xrow, j, s, 4, rcoord[s], second[s])
            forward(j, s, 3)
            forward(j, s, 1)

    def a5(j):
        for s in range(2):
            g_last(xrow, j, s, 4, rcoord[s], second[s])
            forward(j, s, 2)

    def zblock(j):
        return x.at[pl.ds(2 * core, 2), j, yy, xx]

    def z_start():
        for j in range(2):
            send(zblock(j), zblock(j + 2), za_s.at[j], za_r.at[j], far)

    def z_wait(j):
        arrived(zblock(j), za_s.at[j - 2], za_r.at[j - 2], far)

    weights_waited = []

    def m1(j):
        if not weights_waited:
            w_in[0].wait()
            w_in[1].wait()
            weights_waited.append(1)
        forwarded(j)

        @pl.loop(0, 2)
        def _(g):
            t = None
            for q in range(4):
                y_ = jnp.dot(x[q, j].reshape(256, 1024), wgu[g, 1024 * q:1024 * q + 1024, :],
                             preferred_element_type=F32)
                t = y_ if t is None else t + y_
            acc[j, g] = t.reshape(2, 128, 448)
            bsend[j, g] = acc[j, g, 1 - c].astype(BF)
            pltpu.make_async_remote_copy(
                src_ref=bsend.at[j, g], dst_ref=brecv.at[j, g], send_sem=b_s.at[j, g],
                recv_sem=b_r.at[j, g], device_id=pair, device_id_type=MESH).start()

        for g in range(2):
            pending.append(pltpu.make_async_remote_copy(
                src_ref=bsend.at[j, g], dst_ref=brecv.at[j, g], send_sem=b_s.at[j, g],
                recv_sem=b_r.at[j, g], device_id=pair, device_id_type=MESH))

    def hidden(j):
        for g in range(2):
            arrived(brecv.at[j, g], b_s.at[j, g], b_r.at[j, g], pair)
        gate = acc[j, 0, c] + brecv[j, 0].astype(F32)
        up = acc[j, 1, c] + brecv[j, 1].astype(F32)
        hid[j, c] = (gate / (1.0 + jnp.exp(-gate)) * up).astype(BF)
        send(hid.at[j, c], hid.at[j, c], c_s.at[j], c_r.at[j], pair)

    def m2(j):
        if len(weights_waited) == 1:
            for copy in w_in[2:]:
                copy.wait()
            weights_waited.append(1)
        arrived(hid.at[j, 1 - c], c_s.at[j], c_r.at[j], pair)
        for s in range(2):
            h = hid[j].reshape(256, 448)
            psend[j, s] = jnp.dot(h, wdn[2 * other + s], preferred_element_type=F32).astype(BF)
            send(psend.at[j, s], precv.at[j, s], p_s.at[j, s], p_r.at[j, s], mate)

        @pl.loop(0, 2)
        def _(s):
            h = hid[j].reshape(256, 448)
            pown[s] = jnp.dot(h, wdn[2 * core + s], preferred_element_type=F32)

        for s in range(2):
            arrived(precv.at[j, s], p_s.at[j, s], p_r.at[j, s], mate)

            @pl.loop(0, 4)
            def _(r):
                at = pl.ds(pl.multiple_of(64 * r, 64), 64)
                part[j, s, r] = (pown[s, at, :] + precv[j, s, at, :].astype(F32)).astype(BF).reshape(4, 16, 1024)
        r1(part.at[j], j, 0, rxa, ra_s, ra_r, rcoord, second, True)

    def piece(ref, s, r, byrow):
        if not byrow:
            return ref.at[s, r]
        return ref.at[s, r] if s == 0 else ref.at[s, :, r]

    def r1(src, j, base, rx, ss, rs, coord, to, byrow):
        for s in range(2):
            here = coord[s]
            lo, hi, op = (here + 3) % 4, (here + 1) % 4, (here + 2) % 4
            up_, down = to[s][1], to[s][0]
            for slot, which, h, dev in ((0, op, 0, up_), (3, op, 1, down), (1, hi, 1, up_), (4, lo, 0, down)):
                send(cols(piece(src, s, which, byrow), h), rx.at[j, s, slot],
                     ss.at[j, s, slot], rs.at[j, s, slot], dev)

    def r2(src, j, rx, t, ss, rs, coord, to, byrow):
        for s in range(2):
            here = coord[s]
            lo, hi = (here + 3) % 4, (here + 1) % 4
            up_, down = to[s][1], to[s][0]
            for slot, which, h, k, frm, dev in ((0, hi, 0, 2, down, up_), (3, lo, 1, 5, up_, down)):
                arrived(rx.at[j, s, slot], ss.at[j, s, slot], rs.at[j, s, slot], frm)
                own = cols(piece(src, s, which, byrow), h)[...].astype(F32)
                t[j, s, h] = (own + rx[j, s, slot].astype(F32)).astype(BF)
                send(t.at[j, s, h], rx.at[j, s, k], ss.at[j, s, k], rs.at[j, s, k], dev)

    def r3(src, j, rx, ss, rs, coord, to, byrow, s, put):
        here = coord[s]
        for k, frm in ((1, 0), (2, 0), (4, 1), (5, 1)):
            arrived(rx.at[j, s, k], ss.at[j, s, k], rs.at[j, s, k], to[s][frm])
        for h, (a, b) in enumerate(((2, 4), (1, 5))):
            own = cols(piece(src, s, here, byrow), h)[...].astype(F32)
            put(h, own + rx[j, s, a].astype(F32) + rx[j, s, b].astype(F32))

    def ra2(j):
        r2(part.at[j], j, rxa, ta, ra_s, ra_r, rcoord, second, True)

    def ra3(j):
        for s in range(2):
            def put(h, v, s=s):
                ua[j, s, :, :, 512 * h:512 * h + 512] = v.astype(BF)
            r3(part.at[j], j, rxa, ra_s, ra_r, rcoord, second, True, s, put)
        r1(ua.at[j], j, 0, rxb, rb_s, rb_r, pcoord, first, False)

    def rb2(j):
        r2(ua.at[j], j, rxb, tb, rb_s, rb_r, pcoord, first, False)

    def rb3(j):
        for s in range(2):
            def put(h, v, s=s):
                if j < 2:
                    fown[j, s, :, 512 * h:512 * h + 512] = v
                else:
                    zsend[j - 2, s, :, 512 * h:512 * h + 512] = v.astype(BF)
            r3(ua.at[j], j, rxb, rb_s, rb_r, pcoord, first, False, s, put)
        if j >= 2:
            send(zsend.at[j - 2], zrecv.at[j - 2], zr_s.at[j - 2], zr_r.at[j - 2], far)

    def finish():
        for j in range(2):
            arrived(zrecv.at[j], zr_s.at[j], zr_r.at[j], far)
        osend[...] = (fown[other] + zrecv[other].astype(F32)).astype(BF)
        send(osend, orecv, o_s.at[0], o_r.at[0], mate)
        for s in range(2):
            at = pl.ds(pl.multiple_of((2 * core + s) * 1024, 1024), 1024)
            out[:, at] = (fown[core, s] + zrecv[core, s].astype(F32)).astype(BF)
        arrived(orecv, o_s.at[0], o_r.at[0], mate)
        for s in range(2):
            at = pl.ds(pl.multiple_of((2 * other + s) * 1024, 1024), 1024)
            out[:, at] = orecv[s]

    i0, i1, i2, i3 = 0, 2, 3, 1
    z_start()
    a1(0)
    a1(1)
    a2(0)
    a2(1)
    a3(0)
    z_wait(2)
    z_wait(3)
    a1(2)
    a1(3)
    a4(i0)
    a2(i1)
    a2(i2)
    a3(i1)
    a5(i0)
    m1(i0)
    a3(i2)
    a4(i1)
    a5(i1)
    m1(i1)
    hidden(i0)
    a3(i3)
    a4(i2)
    a5(i2)
    m1(i2)
    hidden(i1)
    a4(i3)
    m2(i0)
    a5(i3)
    m1(i3)
    ra2(i0)
    hidden(i2)
    m2(i1)
    ra3(i0)
    ra2(i1)
    rb2(i0)
    hidden(i3)
    m2(i2)
    ra3(i1)
    rb3(i0)
    ra2(i2)
    rb2(i1)
    m2(i3)
    ra3(i2)
    rb3(i1)
    ra2(i3)
    rb2(i2)
    ra3(i3)
    rb3(i2)
    rb2(i3)
    rb3(i3)
    finish()
    for copy in pending:
        copy.wait_send()


def on_device(tokens, norm_gain, gate_weight, up_weight, down_weight):
    dma = pltpu.SemaphoreType.DMA
    pairs = [(4,), (4, 2, 8), (2,), (4, 2, 4), (4, 2), (4,), (4, 2), (4, 2, 6), (4, 2, 6), (2,), (1,)]
    sems = [dma((14,))]
    for shape in pairs:
        sems += [dma(shape), dma(shape)]
    vm = pltpu.VMEM
    any_ = pl.BlockSpec(memory_space=pl.ANY)
    return pl.pallas_call(
        layer,
        out_shape=jax.ShapeDtypeStruct((16, 4096), BF),
        in_specs=[any_] * 5,
        out_specs=pl.BlockSpec(memory_space=pltpu.VMEM),
        scratch_shapes=[
            vm((4, 4, 4, 4, 16, 1024), BF),
            vm((2, 4096, 448), BF),
            vm((4, 448, 1024), BF),
            vm((4, 16, 1024), BF),
            vm((2, 16, 1024), BF),
            vm((4, 1, 1024), F32),
            vm((16, 128), F32),
            vm((3, 16, 128), F32),
            vm((4, 2, 2, 128, 448), F32),
            vm((4, 2, 128, 448), BF),
            vm((4, 2, 128, 448), BF),
            vm((4, 2, 128, 448), BF),
            vm((4, 2, 256, 1024), BF),
            vm((4, 2, 256, 1024), BF),
            vm((2, 256, 1024), F32),
            vm((4, 2, 4, 4, 16, 1024), BF),
            vm((4, 2, 6, 4, 16, 512), BF),
            vm((4, 2, 2, 4, 16, 512), BF),
            vm((4, 2, 4, 16, 1024), BF),
            vm((4, 2, 6, 16, 512), BF),
            vm((4, 2, 2, 16, 512), BF),
            vm((2, 2, 16, 1024), F32),
            vm((2, 2, 16, 1024), BF),
            vm((2, 2, 16, 1024), BF),
            vm((2, 16, 1024), BF),
            vm((2, 16, 1024), BF),
            *sems,
        ],
        compiler_params=pltpu.CompilerParams(
            collective_id=0, has_side_effects=True, vmem_limit_bytes=62 * 1024 * 1024),
    )(tokens, norm_gain.reshape(1, -1), gate_weight, up_weight, down_weight)


def solution(mesh):
    placed = (P("row", "col"), P("col"), P("col", "row"), P("col", "row"), P("row", "col"))
    return jax.shard_map(
        on_device, mesh=mesh, in_specs=placed, out_specs=P("row", "col"), check_vma=False
    )
```

time: 436 us -> 117 us (0.27)
  waiting for transfers between devices: 321 us -> 0 us
  Pallas kernels: 0 us -> 101 us
  blocking collectives: 67.4 us -> 0 us
  matrix products: 18.2 us -> 0 us
  between operations: 13.2 us -> 0.01 us
  other arithmetic: 7.72 us -> 0 us
  local copies, waits for them, and re-layouts: 7.32 us -> 14.5 us
    reduce_scatter x2 -> x0, waiting for transfers between devices: 236 us -> none  [the longest x1 211 us: summed_rows(): return lax.psum_scatter(blocks, chips, scatter_dimension=0, tiled=True)[0]]
    pallas_call x0 -> x1, Pallas kernels: none -> 101 us  [on_device(): pl.pallas_call(layer, out_shape=jax.ShapeDtypeStruct((16, 4096), BF), in_...]
    all_gather x1 -> x0, waiting for transfers between devices: 85.4 us -> none  [on_device(): piece = lax.all_gather(normed, ROW, axis=0, tiled=True)]
    all_to_all x3 -> x0, blocking collectives: 67.4 us -> none  [the longest x1 46 us: sum_at_owner(): blocks = lax.all_to_all(in_blocks(x, dim, count), axis, 0, 0, tiled=True)]
    dot_general x3 -> x0, matrix products: 18.2 us -> none  [the longest x1 7.65 us: on_device(): up_part = jnp.dot(piece, up_weight, preferred_element_type=jnp.float32)]
    unnamed x4 -> x3, local copies, waits for them, and re-layouts: 0.25 us -> 14.5 us
    transpose x1 -> x0, local copies, waits for them, and re-layouts: 6.03 us -> none  [summed_rows(): blocks = blocks.reshape(*sizes, *inside).swapaxes(0, 1).reshape(-1, *inside)]
  transfers between devices with their start and end apart: 3 -> 0, of which waited for: 3 -> 0; matrix products, arithmetic and copies ran while one was open for 0% -> 0% of each run, Pallas kernels for 0% -> 0%
where the time goes in v1:
time: 117 us; the launch traced here: 115 us
  Pallas kernels  101 us (86%)
  local copies, waits for them, and re-layouts  14.5 us (12%)
    pallas_call x1, Pallas kernels, on_device(): pl.pallas_call(layer, out_shape=jax.ShapeDtypeStruct((16, 4096), BF), in_...  101 us
    unnamed x3, local copies, waits for them, and re-layouts  14.5 us

profile of v1, /device:TPU:0, one launch (start us, length us, event | category | flops | bytes accessed | tf_op | source)
XLA Modules:
  0.0 115.3 jit_solution(13603539092632964177)
XLA Ops:
  0.0 6.4 %copy.6.wg = bf16[4096,448]{1,0:T(8,128)(2,1)} copy(bf16[4096,448]{0,1:T(8,128)(2,1)} %param.7) | data formatting | bytes 7340032 | tf_op args[2]
  6.4 6.5 %copy.7.wu = bf16[4096,448]{1,0:T(8,128)(2,1)} copy(bf16[4096,448]{0,1:T(8,128)(2,1)} %param.8) | data formatting | bytes 7340032 | tf_op args[3]
  12.9 100.8 %shard_map.55 = bf16[16,4096]{1,0:T(8,128)(2,1)} custom-call(bf16[16,4096]{1,0:T(8,128)(2,1)} %tok.1, f32[1,4096]{1,0:T(1,128)} %bitcast.1, bf16[4096,448]{1,0:T(8,128)(2,1)} %copy.6.wg, bf16[4096,448]{1,0:T(8,128)(2,1)} %copy.7.wu, bf16[448,4096]{1,0:T(8,128)(2,1)} %wd.1), custom_call_target="tpu_custom_call" | custom-call | tf_op jit(solution)/shard_map/pallas_call | solution.py:372
  113.8 1.6 %copy.9 = bf16[16,4096]{1,0:T(8,128)(2,1)} copy(bf16[16,4096]{1,0:T(8,128)(2,1)} %shard_map.55) | data formatting | bytes 262144

commit v2 on v1

--- a/solution.py
+++ b/solution.py
@@ -187,8 +187,8 @@
         def _(g):
             t = None
             for q in range(4):
-                y_ = jnp.dot(x[q, j].reshape(256, 1024), wgu[g, 1024 * q:1024 * q + 1024, :],
-                             preferred_element_type=F32)
+                y_ = lax.dot_general(x[q, j].reshape(256, 1024), wgu[g, :, 1024 * q:1024 * q + 1024],
+                                     (((1,), (1,)), ((), ())), preferred_element_type=F32)
                 t = y_ if t is None else t + y_
             acc[j, g] = t.reshape(2, 128, 448)
             bsend[j, g] = acc[j, g, 1 - c].astype(BF)
@@ -376,7 +376,7 @@
         out_specs=pl.BlockSpec(memory_space=pltpu.VMEM),
         scratch_shapes=[
             vm((4, 4, 4, 4, 16, 1024), BF),
-            vm((2, 4096, 448), BF),
+            vm((2, 448, 4096), BF),
             vm((4, 448, 1024), BF),
             vm((4, 16, 1024), BF),
             vm((2, 16, 1024), BF),
@@ -405,7 +405,7 @@
         ],
         compiler_params=pltpu.CompilerParams(
             collective_id=0, has_side_effects=True, vmem_limit_bytes=62 * 1024 * 1024),
-    )(tokens, norm_gain.reshape(1, -1), gate_weight, up_weight, down_weight)
+    )(tokens, norm_gain.reshape(1, -1), gate_weight.T, up_weight.T, down_weight)
 
 
 def solution(mesh):

time: 117 us -> 104 us (0.89)
  local copies, waits for them, and re-layouts: 14.5 us -> 1.57 us
    unnamed x3 -> x1, local copies, waits for them, and re-layouts: 14.5 us -> 1.57 us
where the time goes in v2:
time: 104 us; the launch traced here: 102 us
  Pallas kernels  101 us (97%)
  local copies, waits for them, and re-layouts  1.57 us (2%)
    pallas_call x1, Pallas kernels, on_device(): pl.pallas_call(layer, out_shape=jax.ShapeDtypeStruct((16, 4096), BF), in_...  101 us

profile of v2, /device:TPU:0, one launch (start us, length us, event | category | flops | bytes accessed | tf_op | source)
XLA Modules:
  0.0 102.4 jit_solution(3222791461478543587)
XLA Ops:
  0.0 100.8 %shard_map.55 = bf16[16,4096]{1,0:T(8,128)(2,1)} custom-call(bf16[16,4096]{1,0:T(8,128)(2,1)} %tok.1, f32[1,4096]{1,0:T(1,128)} %bitcast.5, bf16[448,4096]{1,0:T(8,128)(2,1)} %bitcast.3, bf16[448,4096]{1,0:T(8,128)(2,1)} %bitcast.4, bf16[448,4096]{1,0:T(8,128)(2,1)} %wd.1), custom_call_target="tpu_custom_call" | custom-call | tf_op jit(solution)/shard_map/pallas_call | solution.py:372
  100.8 1.6 %copy.7 = bf16[16,4096]{1,0:T(8,128)(2,1)} copy(bf16[16,4096]{1,0:T(8,128)(2,1)} %shard_map.55) | data formatting | bytes 262144
